TPU v7x, 16 devices: a whole 2x2x2 slice. The times are simulated.
16 devices in a mesh: rep: 1, dp: 16 (over x, y, z, core).
Axes of the slice: x: 2, y: 2, z: 2, core: 2. Of those that a mesh axis runs over, the one named last changes fastest.
Arguments:
- g_w_gate: bfloat16 [16, 2, 512, 8192], P(('rep', 'dp'))
- g_w_up: bfloat16 [16, 2, 512, 8192], P(('rep', 'dp'))
- g_w_down: bfloat16 [16, 2, 8192, 512], P(('rep', 'dp'))
- w_gate: bfloat16 [2, 512, 8192], replicated
- w_up: bfloat16 [2, 512, 8192], replicated
- w_down: bfloat16 [2, 8192, 512], replicated
- m_w_gate: float32 [2, 512, 8192], P(None, 'dp')
- m_w_up: float32 [2, 512, 8192], P(None, 'dp')
- m_w_down: float32 [2, 8192, 512], P(None, 'dp')
- v_w_gate: float32 [2, 512, 8192], P(None, 'dp')
- v_w_up: float32 [2, 512, 8192], P(None, 'dp')
- v_w_down: float32 [2, 8192, 512], P(None, 'dp')
Outputs:
- output 1: bfloat16 [2, 512, 8192], P('rep')
- output 2: bfloat16 [2, 512, 8192], P('rep')
- output 3: bfloat16 [2, 8192, 512], P('rep')
- output 4: float32 [2, 512, 8192], P('rep', 'dp')
- output 5: float32 [2, 512, 8192], P('rep', 'dp')
- output 6: float32 [2, 8192, 512], P('rep', 'dp')
- output 7: float32 [2, 512, 8192], P('rep', 'dp')
- output 8: float32 [2, 512, 8192], P('rep', 'dp')
- output 9: float32 [2, 8192, 512], P('rep', 'dp')
All inputs are finite; a program needn't handle non-finite values.
Results may differ from a plain program's by a relative error of at most 0.022.
Values are sent between devices in bfloat16 or wider.
A program may use at most 2 GiB of HBM per device.

v0:
```python
import jax
import jax.numpy as jnp
from jax import lax
from jax.sharding import PartitionSpec as P


def adamw(w, m, v, g):
    m = 0.9 * m + 0.1 * g
    v = 0.95 * v + 0.05 * g * g
    step = m * lax.rsqrt(v + 1e-8) + 0.1 * w
    return (w - 0.02 * step).astype(jnp.bfloat16), m, v


def solution(mesh):
    def step(*arrays):
        terms, weights, m, v = (arrays[i : i + 3] for i in (0, 3, 6, 9))
        gradients = [lax.psum_scatter(t[0], "dp", scatter_dimension=1, tiled=True).astype(jnp.float32) for t in terms]
        me = lax.axis_index("dp")
        own = [lax.dynamic_slice_in_dim(w, me * one.shape[1], one.shape[1], 1).astype(jnp.float32) for w, one in zip(weights, m, strict=True)]
        new = [adamw(w, m, v, g) for w, m, v, g in zip(own, m, v, gradients, strict=True)]
        whole = [lax.all_gather(one[0], "dp", axis=1, tiled=True) for one in new]
        return (*whole, *(one[1] for one in new), *(one[2] for one in new))

    all_of, cut = P(None, None, None), P(None, "dp", None)
    return jax.shard_map(
        step,
        mesh=mesh,
        in_specs=(P(("rep", "dp"), None, None, None),) * 3 + (all_of,) * 3 + (cut,) * 6,
        out_specs=(P("rep", None, None),) * 3 + (P("rep", "dp", None),) * 6,
        check_vma=False,
    )
```

profile of v0, /device:TPU:0, one launch (start us, length us, event | category | flops | bytes accessed | tf_op | source)
XLA Modules:
  0.0 823.0 jit_solution(2866139980504800513)
XLA Ops:
  7.2 0.0 reduce-scatter.8.cloned.1.call-start
  7.2 0.7 reduce-scatter.8.cloned.1.call-update
  7.9 0.0 reduce-scatter.6.cloned.1.call-start
  8.0 0.7 reduce-scatter.6.cloned.1.call-update
  8.7 0.0 reduce-scatter.4.cloned.1.call-start
  8.7 0.0 copy-start.1
  8.7 0.7 reduce-scatter.4.cloned.1.call-update
  9.4 0.0 all-gather.8.cloned.1.call-start
  9.4 175.7 %reduce-scatter.8.cloned.1.call-done = bf16[2,512,512]{2,1,0:T(8,128)(2,1)} async-done(((bf16[2,8192,512]{2,1,0:T(8,128)(2,1)}), bf16[2,512,512]{2,1,0:T(8,128)(2,1)}) %reduce-scatter.8.cloned.1.call-update) | async-done | bytes 1048592 | tf_op jit(solution)/shard_map/reduce_scatter | solution.py:17
  185.2 0.0 copy-done.1
  185.2 5.3 fusion.10
  190.4 0.0 all-gather.8.cloned.1.call-update
  190.5 0.0 all-gather.6.cloned.1.call-start
  190.5 173.0 %reduce-scatter.6.cloned.1.call-done = bf16[2,32,8192]{2,1,0:T(8,128)(2,1)} async-done(((bf16[2,512,8192]{2,1,0:T(8,128)(2,1)}), bf16[2,32,8192]{2,1,0:T(8,128)(2,1)}) %reduce-scatter.6.cloned.1.call-update) | async-done | bytes 1048592 | tf_op jit(solution)/shard_map/reduce_scatter | solution.py:17
  363.5 0.0 copy-start.2
  363.5 5.9 fusion.6
  369.4 0.0 all-gather.6.cloned.1.call-update
  369.4 0.0 all-gather.4.cloned.1.call-start
  369.4 172.4 %reduce-scatter.4.cloned.1.call-done = bf16[2,32,8192]{2,1,0:T(8,128)(2,1)} async-done(((bf16[2,512,8192]{2,1,0:T(8,128)(2,1)}), bf16[2,32,8192]{2,1,0:T(8,128)(2,1)}) %reduce-scatter.4.cloned.1.call-update) | async-done | bytes 1048592 | tf_op jit(solution)/shard_map/reduce_scatter | solution.py:17
  541.9 0.0 copy-done.2
  541.9 5.1 fusion.2
  547.0 0.0 all-gather.4.cloned.1.call-update
  547.0 77.7 %all-gather.8.cloned.1.call-done = bf16[2,8192,512]{2,1,0:T(8,128)(2,1)} async-done(((bf16[2,512,512]{2,1,0:T(8,128)(2,1)}), bf16[2,8192,512]{2,1,0:T(8,128)(2,1)}) %all-gather.8.cloned.1.call-update) | async-done | bytes 16777232 | tf_op jit(solution)/shard_map/all_gather | solution.py:21
  624.6 78.7 %all-gather.6.cloned.1.call-done = bf16[2,512,8192]{2,1,0:T(8,128)(2,1)} async-done(((bf16[2,32,8192]{2,1,0:T(8,128)(2,1)}), bf16[2,512,8192]{2,1,0:T(8,128)(2,1)}) %all-gather.6.cloned.1.call-update) | async-done | bytes 16777232 | tf_op jit(solution)/shard_map/all_gather | solution.py:21
  703.4 78.8 %all-gather.4.cloned.1.call-done = bf16[2,512,8192]{2,1,0:T(8,128)(2,1)} async-done(((bf16[2,32,8192]{2,1,0:T(8,128)(2,1)}), bf16[2,512,8192]{2,1,0:T(8,128)(2,1)}) %all-gather.4.cloned.1.call-update) | async-done | bytes 16777232 | tf_op jit(solution)/shard_map/all_gather | solution.py:21
  782.1 0.0 copy-start
  782.1 0.0 slice-start
  782.1 0.0 slice-start.1
  782.1 16.7 %copy.24 = bf16[2,512,8192]{2,1,0:T(8,128)(2,1)} copy(bf16[2,512,8192]{2,1,0:T(8,128)(2,1)} %all-gather.4.cloned.1.call-done) | data formatting | bytes 33554432
  798.8 0.0 copy-done
  798.8 0.0 slice-start.2
  798.8 0.0 slice-start.3
  798.8 8.5 %copy.25 = bf16[2,512,8192]{2,1,0:T(8,128)(2,1)} copy(bf16[2,512,8192]{2,1,0:T(8,128)(2,1)S(1)} %copy-done) | data formatting | bytes 33554432
  807.3 0.0 slice-done
  807.3 0.0 slice-done.1
  807.3 1.5 slice-done.2
  808.8 1.2 slice-done.3
  810.0 6.2 copy.26
  (1 shorter events, 0.0 us)
Async XLA Ops:
  7.2 178.0 %reduce-scatter.8.cloned.1.call-start = ((), (), s32[]{:S(2)}) async-start(), calls=%async_computation.7 | async-start | bytes 17825792 | tf_op jit(solution)/shard_map/reduce_scatter | solution.py:17
  7.9 355.6 %reduce-scatter.6.cloned.1.call-start = ((), (), s32[]{:S(2)}) async-start(), calls=%async_computation.5 | async-start | bytes 17825792 | tf_op jit(solution)/shard_map/reduce_scatter | solution.py:17
  8.7 533.2 %reduce-scatter.4.cloned.1.call-start = ((), (), s32[]{:S(2)}) async-start(), calls=%async_computation.3 | async-start | bytes 17825792 | tf_op jit(solution)/shard_map/reduce_scatter | solution.py:17
  8.7 176.5 %copy-start.1 = (f32[2,512,512]{2,1,0:T(8,128)S(1)}, f32[2,512,512]{2,1,0:T(8,128)}, u32[]{:S(2)}) copy-start(f32[2,512,512]{2,1,0:T(8,128)} %param.23) | copy-start | bytes 6291460
  9.4 615.2 %all-gather.8.cloned.1.call-start = ((), (), s32[]{:S(2)}) async-start(), calls=%async_computation.8 | async-start | bytes 17825792 | tf_op jit(solution)/shard_map/all_gather | solution.py:21
  190.5 512.9 %all-gather.6.cloned.1.call-start = ((), (), s32[]{:S(2)}) async-start(), calls=%async_computation.6 | async-start | bytes 17825792 | tf_op jit(solution)/shard_map/all_gather | solution.py:21
  363.5 178.4 %copy-start.2 = (f32[2,32,8192]{2,1,0:T(8,128)S(1)}, f32[2,32,8192]{2,1,0:T(8,128)}, u32[]{:S(2)}) copy-start(f32[2,32,8192]{2,1,0:T(8,128)} %param.21) | copy-start | bytes 6291460
  369.4 412.7 %all-gather.4.cloned.1.call-start = ((), (), s32[]{:S(2)}) async-start(), calls=%async_computation.4 | async-start | bytes 17825792 | tf_op jit(solution)/shard_map/all_gather | solution.py:21
  782.1 16.7 %copy-start = (bf16[2,512,8192]{2,1,0:T(8,128)(2,1)S(1)}, bf16[2,512,8192]{2,1,0:T(8,128)(2,1)}, u32[]{:S(2)}) copy-start(bf16[2,512,8192]{2,1,0:T(8,128)(2,1)} %all-gather.6.cloned.1.call-done) | copy-start | bytes 50331652
  782.1 25.2 %slice-start = ((s8[16777216]{0:T(1024)(128)(4,1)}), s8[4194304]{0:T(1024)(128)(4,1)S(1)}, s32[]{:S(2)}) async-start(s8[16777216]{0:T(1024)(128)(4,1)} %bitcast.6), calls=%async_computation.9 | async-start | bytes 8388608
  782.1 25.2 %slice-start.1 = ((s8[16777216]{0:T(1024)(128)(4,1)}), s8[4194304]{0:T(1024)(128)(4,1)S(1)}, s32[]{:S(2)}) async-start(s8[16777216]{0:T(1024)(128)(4,1)} %bitcast.6), calls=%async_computation.10 | async-start | bytes 8388608
  798.8 10.0 %slice-start.2 = ((s8[16777216]{0:T(1024)(128)(4,1)}), s8[4194304]{0:T(1024)(128)(4,1)S(1)}, s32[]{:S(2)}) async-start(s8[16777216]{0:T(1024)(128)(4,1)} %bitcast.6), calls=%async_computation.11 | async-start | bytes 8388608
  798.8 11.2 %slice-start.3 = ((s8[16777216]{0:T(1024)(128)(4,1)}), s8[4194304]{0:T(1024)(128)(4,1)S(1)}, s32[]{:S(2)}) async-start(s8[16777216]{0:T(1024)(128)(4,1)} %bitcast.6), calls=%async_computation.12 | async-start | bytes 8388608
Sparse Core Ops, SparseCore 0:
  10.3 174.8 reduce-scatter.7
  187.4 176.0 reduce-scatter.5
  365.8 176.0 reduce-scatter.3
  544.6 80.0 all-gather.7
  627.3 76.0 all-gather.5
  706.1 76.0 all-gather.3
where the time goes:
time: 823 us
  waiting for transfers between devices  758 us (92%)
  local copies, waits for them, and re-layouts  34.1 us (4%)
  other arithmetic  16.2 us (2%)
  between operations  14.1 us (2%)
    reduce_scatter x3, waiting for transfers between devices, step(): lax.psum_scatter(t[0], 'dp', scatter_dimension=1, tiled=True)  521 us
    all_gather x3, waiting for transfers between devices, step(): whole = [lax.all_gather(one[0], 'dp', axis=1, tiled=True) for one in new]  235 us
    unnamed x17, local copies, waits for them, and re-layouts  34.1 us
  transfers between devices with their start and end apart: 6, of which 6 were waited for; matrix products, arithmetic and copies ran while one was open for 2% of the time, Pallas kernels for 0%

commit v1 on v0

v1 whole, which is shorter than its diff:
```python
import functools

import jax
import jax.numpy as jnp
from jax import lax
from jax.experimental import pallas as pl
from jax.experimental.pallas import tpu as pltpu
from jax.sharding import PartitionSpec as P

SUB = 4
LAYERS = 2
J = LAYERS * SUB
AHEAD = 2
STRIDE = {"x": 8, "y": 4, "z": 2}
ORDER = (("x", "y", "z"), ("y", "z", "x"), ("z", "x", "y"))
C = 3
F32, BF16 = jnp.float32, jnp.bfloat16
MESH = pl.DeviceIdType.MESH
D0, S1, S2, S3, A1, A2, A3, FW = range(8)


def adamw(w, m, v, g):
    m = 0.9 * m + 0.1 * g
    v = 0.95 * v + 0.05 * g * g
    step = m * lax.rsqrt(v + 1e-8) + 0.1 * w
    return (w - 0.02 * step).astype(BF16), m, v


def kernel(*refs):
    it = iter(refs)

    def take(n=C):
        return [next(it) for _ in range(n)]

    g, w, m, v = take(), take(), take(), take()
    out, m_out, v_out = take(), take(), take()
    r0, r1, r2, r3 = take(), take(), take(), take()
    o1, o2, o3, o4 = take(), take(), take(), take()
    mb, vb, wb = take(), take(), take()
    send, recv, local, load, moved = take(5)

    me = lax.axis_index("dp")
    core = me % 2
    bit = {d: me // s % 2 for d, s in STRIDE.items()}
    near = {d: me + s * (1 - 2 * bit[d]) for d, s in STRIDE.items()}
    partner = me + 1 - 2 * core
    mine = [tuple(bit[d] for d in ORDER[c]) for c in range(C)]

    def block(c, b0, b1, b2, k):
        s = [STRIDE[d] for d in ORDER[c]]
        return b0 * s[0] + b1 * s[1] + b2 * s[2] + k

    def part(c, j):
        layer, s = j // SUB, j % SUB
        if c < 2:
            width = 8192 // SUB
            return layer, slice(None), pl.ds(pl.multiple_of(s * width, width), width)
        height = 512 // SUB
        return layer, pl.ds(pl.multiple_of(s * height, height), height), slice(None)

    def of_block(ref, c, blk, j):
        layer, rows, columns = part(c, j)
        return ref.at[layer, blk, rows, columns]

    def of_own(ref, c, j):
        layer, rows, columns = part(c, j)
        return ref.at[layer, rows, columns]

    def remote(c, j, group, src, dst, to):
        return pltpu.make_async_remote_copy(
            src_ref=src, dst_ref=dst, send_sem=send.at[group, c, j], recv_sem=recv.at[group, c, j], device_id={"dp": to}, device_id_type=MESH
        )

    def wait_for(ref, sem):
        pltpu.make_async_copy(ref, ref, sem).wait()

    def tiles(c, body, rows=32):
        if c < 2:
            across, down, high = 8192 // SUB // 512, 32 // rows, rows
        else:
            across, down = 1, 512 // SUB // rows

        @pl.loop(0, across * down)
        def _(i):
            row = pl.multiple_of(i % down * rows, rows)
            column = pl.multiple_of(i // down * 512, 512)
            body((pl.ds(row, rows), pl.ds(column, 512)))

    def start_exchange(j):
        for c in range(C):
            for p in range(8):
                blk = block(c, p // 4, p // 2 % 2, p % 2, 1 - core)
                remote(c, j, D0, of_block(g[c], c, blk, j), r0[c].at[j, p], partner).start()

    def load_terms(stage, j):
        slot = j % 2
        for c in range(C):
            m0, m1, m2 = mine[c]
            if stage == 0:
                places = [(1 - m0, q // 2, q % 2) for q in range(4)]
            elif stage == 1:
                places = [(m0, 1 - m1, q) for q in range(2)]
            elif stage == 2:
                places = [(m0, m1, 1 - m2)]
            else:
                places = [(m0, m1, m2)]
            to = (o1, o2, o3, o4)[stage][c]
            for q, place in enumerate(places):
                pltpu.make_async_copy(of_block(g[c], c, block(c, *place, core), j), to.at[slot, q], load.at[stage, c, slot]).start()

    def load_own(j):
        slot = j % 2
        for c in range(C):

            @pl.when(j >= 2)
            def _():
                wait_for(mb[c].at[slot], moved.at[0, c, slot])
                wait_for(vb[c].at[slot], moved.at[1, c, slot])

            pltpu.make_async_copy(of_own(m[c], c, j), mb[c].at[slot], load.at[4, c, slot]).start()
            pltpu.make_async_copy(of_own(v[c], c, j), vb[c].at[slot], load.at[5, c, slot]).start()
            pltpu.make_async_copy(of_block(w[c], c, me, j), wb[c].at[slot], load.at[6, c, slot]).start()

    def stage1(j):
        slot = j % 2
        for c in range(C):
            m0, m1, m2 = mine[c]
            wait_for(r0[c].at[j], recv.at[D0, c, j])
            wait_for(o1[c].at[slot], load.at[0, c, slot])

            def body(at):
                for q in range(4):
                    p = (1 - m0) * 4 + q
                    r0[c][(j, p, *at)] = (r0[c][(j, p, *at)].astype(F32) + o1[c][(slot, q, *at)].astype(F32)).astype(BF16)

            tiles(c, body)
            remote(c, j, S1, r0[c].at[j, pl.ds((1 - m0) * 4, 4)], r1[c].at[j], near[ORDER[c][0]]).start()

    def stage2(j):
        slot = j % 2
        for c in range(C):
            m0, m1, m2 = mine[c]
            wait_for(o2[c].at[slot], load.at[1, c, slot])
            wait_for(r1[c].at[j], recv.at[S1, c, j])
            wait_for(r1[c].at[j], send.at[S1, c, j])

            def body(at):
                for q in range(2):
                    p = (1 - m1) * 2 + q
                    total = r0[c][(j, m0 * 4 + p, *at)].astype(F32) + o2[c][(slot, q, *at)].astype(F32)
                    r1[c][(j, p, *at)] = (total + r1[c][(j, p, *at)].astype(F32)).astype(BF16)

            tiles(c, body)
            remote(c, j, S2, r1[c].at[j, pl.ds((1 - m1) * 2, 2)], r2[c].at[j], near[ORDER[c][1]]).start()

    def stage3(j):
        slot = j % 2
        for c in range(C):
            m0, m1, m2 = mine[c]
            wait_for(o3[c].at[slot], load.at[2, c, slot])
            wait_for(r2[c].at[j], recv.at[S2, c, j])
            wait_for(r2[c].at[j], send.at[S2, c, j])

            def body(at):
                p = 1 - m2
                total = r0[c][(j, m0 * 4 + m1 * 2 + p, *at)].astype(F32) + o3[c][(slot, 0, *at)].astype(F32)
                total = total + r1[c][(j, m1 * 2 + p, *at)].astype(F32)
                r2[c][(j, p, *at)] = (total + r2[c][(j, p, *at)].astype(F32)).astype(BF16)

            tiles(c, body)
            remote(c, j, S3, r2[c].at[j, pl.ds(1 - m2, 1)], r3[c].at[j], near[ORDER[c][2]]).start()

    def give(c, j, p, n):
        for q in range(n):
            at = p + q
            to = of_block(out[c], c, block(c, at // 4, at // 2 % 2, at % 2, core), j)
            remote(c, j, FW, r0[c].at[j, at], to, partner).start()
            pltpu.make_async_copy(r0[c].at[j, at], to, local.at[c, j]).start()

    def stage4(j):
        slot = j % 2
        for c in range(C):
            m0, m1, m2 = mine[c]
            here = m0 * 4 + m1 * 2 + m2
            wait_for(o4[c].at[slot], load.at[3, c, slot])
            wait_for(mb[c].at[slot], load.at[4, c, slot])
            wait_for(vb[c].at[slot], load.at[5, c, slot])
            wait_for(wb[c].at[slot], load.at[6, c, slot])
            wait_for(r3[c].at[j], recv.at[S3, c, j])
            wait_for(r3[c].at[j], send.at[S3, c, j])

            def body(at):
                total = r0[c][(j, here, *at)].astype(F32) + o4[c][(slot, 0, *at)].astype(F32)
                total = total + r1[c][(j, m1 * 2 + m2, *at)].astype(F32)
                total = total + r2[c][(j, m2, *at)].astype(F32)
                total = total + r3[c][(j, 0, *at)].astype(F32)
                grad = total.astype(BF16).astype(F32)
                new = adamw(wb[c][(slot, *at)].astype(F32), mb[c][(slot, *at)], vb[c][(slot, *at)], grad)
                r0[c][(j, here, *at)], mb[c][(slot, *at)], vb[c][(slot, *at)] = new

            tiles(c, body, rows=16)
            remote(c, j, A1, r0[c].at[j, here], r0[c].at[j, here], near[ORDER[c][2]]).start()
            pltpu.make_async_copy(mb[c].at[slot], of_own(m_out[c], c, j), moved.at[0, c, slot]).start()
            pltpu.make_async_copy(vb[c].at[slot], of_own(v_out[c], c, j), moved.at[1, c, slot]).start()
            give(c, j, here, 1)

    def stage5(j):
        for c in range(C):
            m0, m1, m2 = mine[c]
            pair = m0 * 4 + m1 * 2
            wait_for(r3[c].at[j], recv.at[A1, c, j])
            remote(c, j, A2, r0[c].at[j, pl.ds(pair, 2)], r0[c].at[j, pl.ds(pair, 2)], near[ORDER[c][1]]).start()
            give(c, j, pair + 1 - m2, 1)

    def stage6(j):
        for c in range(C):
            m0, m1, m2 = mine[c]
            wait_for(r2[c].at[j], recv.at[A2, c, j])
            remote(c, j, A3, r0[c].at[j, pl.ds(m0 * 4, 4)], r0[c].at[j, pl.ds(m0 * 4, 4)], near[ORDER[c][0]]).start()
            give(c, j, m0 * 4 + (1 - m1) * 2, 2)

    def stage7(j):
        for c in range(C):
            m0, m1, m2 = mine[c]
            wait_for(r1[c].at[j], recv.at[A3, c, j])
            give(c, j, (1 - m0) * 4, 4)

    barrier = pltpu.get_barrier_semaphore()
    for to in (partner, *near.values()):
        pl.semaphore_signal(barrier, inc=1, device_id={"dp": to}, device_id_type=MESH)
    pl.semaphore_wait(barrier, 4)

    for j in range(AHEAD):
        start_exchange(j)
    load_terms(0, 0)

    @pl.loop(0, J + 6)
    def _(t):
        def on(j, run):
            pl.when(jnp.logical_and(j >= 0, j < J))(lambda: run(j))

        on(t + AHEAD, start_exchange)
        on(t + 1, functools.partial(load_terms, 0))
        on(t, functools.partial(load_terms, 1))
        on(t - 1, functools.partial(load_terms, 2))
        on(t - 2, functools.partial(load_terms, 3))
        on(t - 2, load_own)
        for back, stage in enumerate((stage1, stage2, stage3, stage4, stage5, stage6, stage7)):
            on(t - back, stage)

    for c in range(C):
        for slot in range(2):
            wait_for(mb[c].at[slot], moved.at[0, c, slot])
            wait_for(vb[c].at[slot], moved.at[1, c, slot])

    @pl.loop(0, J)
    def _(j):
        for c in range(C):
            wait_for(r0[c].at[j], send.at[D0, c, j])
            wait_for(r3[c].at[j], send.at[A1, c, j])
            wait_for(r2[c].at[j], send.at[A2, c, j])
            wait_for(r1[c].at[j], send.at[A3, c, j])
            wait_for(r0[c].at[j], local.at[c, j])
            wait_for(r0[c].at[j], send.at[FW, c, j])
            wait_for(r0[c].at[j], recv.at[FW, c, j])


def solution(mesh):
    chunk = ((32, 8192 // SUB),) * 2 + ((512 // SUB, 512),)
    blocks = ((LAYERS, 16, 32, 8192),) * 2 + ((LAYERS, 16, 512, 512),)
    own = ((LAYERS, 32, 8192),) * 2 + ((LAYERS, 512, 512),)
    whole = ((LAYERS, 512, 8192),) * 2 + ((LAYERS, 8192, 512),)

    def vmem(*lead, dtype=BF16):
        return [pltpu.VMEM((*lead, *chunk[c]), dtype) for c in range(C)]

    call = pl.pallas_call(
        kernel,
        out_shape=[jax.ShapeDtypeStruct(s, BF16) for s in blocks] + [jax.ShapeDtypeStruct(s, F32) for s in own] * 2,
        in_specs=[pl.BlockSpec(memory_space=pl.ANY)] * 12,
        out_specs=[pl.BlockSpec(memory_space=pl.ANY)] * 9,
        scratch_shapes=[
            *vmem(J, 8),
            *vmem(J, 4),
            *vmem(J, 2),
            *vmem(J, 1),
            *vmem(2, 4),
            *vmem(2, 2),
            *vmem(2, 1),
            *vmem(2, 1),
            *vmem(2, dtype=F32),
            *vmem(2, dtype=F32),
            *vmem(2),
            pltpu.SemaphoreType.DMA((8, C, J)),
            pltpu.SemaphoreType.DMA((8, C, J)),
            pltpu.SemaphoreType.DMA((C, J)),
            pltpu.SemaphoreType.DMA((7, C, 2)),
            pltpu.SemaphoreType.DMA((2, C, 2)),
        ],
        compiler_params=pltpu.CompilerParams(collective_id=0, has_side_effects=True, vmem_limit_bytes=67043328),
    )

    def step(*arrays):
        terms = [a.reshape(s) for a, s in zip(arrays[:3], blocks, strict=True)]
        weights = [a.reshape(s) for a, s in zip(arrays[3:6], blocks, strict=True)]
        new = call(*terms, *weights, *arrays[6:])
        return (*(a.reshape(s) for a, s in zip(new[:3], whole, strict=True)), *new[3:])

    all_of, cut = P(None, None, None), P(None, "dp", None)
    return jax.shard_map(
        step,
        mesh=mesh,
        in_specs=(P(("rep", "dp"), None, None, None),) * 3 + (all_of,) * 3 + (cut,) * 6,
        out_specs=(P("rep", None, None),) * 3 + (P("rep", "dp", None),) * 6,
        check_vma=False,
    )
```

time: 823 us -> 380 us (0.46)
  waiting for transfers between devices: 758 us -> 0 us
  Pallas kernels: 0 us -> 331 us
  other arithmetic: 16.2 us -> 0.01 us
  between operations: 14.1 us -> 0.7 us
  local copies, waits for them, and re-layouts: 34.1 us -> 47.2 us
    reduce_scatter x3 -> x0, waiting for transfers between devices: 521 us -> none  [step(): lax.psum_scatter(t[0], 'dp', scatter_dimension=1, tiled=True)]
    pallas_call x0 -> x1, Pallas kernels: none -> 331 us  [step(): new = call(*terms, *weights, *arrays[6:])]
    all_gather x3 -> x0, waiting for transfers between devices: 235 us -> none  [step(): whole = [lax.all_gather(one[0], 'dp', axis=1, tiled=True) for one in new]]
    convert_element_type x3 -> x0, other arithmetic: 16.2 us -> none  [adamw(): return ((w - 0.02 * step).astype(jnp.bfloat16), m, v)]
    unnamed x17 -> x31, local copies, waits for them, and re-layouts: 34.1 us -> 47.2 us
  transfers between devices with their start and end apart: 6 -> 0, of which waited for: 6 -> 0; matrix products, arithmetic and copies ran while one was open for 2% -> 0% of each run, Pallas kernels for 0% -> 0%
where the time goes in v1:
time: 380 us; the launch traced here: 379 us
  Pallas kernels  331 us (87%)
  local copies, waits for them, and re-layouts  47.2 us (12%)
    pallas_call x1, Pallas kernels, step(): new = call(*terms, *weights, *arrays[6:])  331 us
    unnamed x31, local copies, waits for them, and re-layouts  47.2 us

profile of v1, /device:TPU:0, one launch (start us, length us, event | category | flops | bytes accessed | tf_op | source)
XLA Modules:
  0.0 379.2 jit_solution(9566222584404124103)
XLA Ops:
  0.6 331.3 %shard_map.187 = (bf16[2,16,32,8192]{3,2,1,0:T(8,128)(2,1)}, bf16[2,16,32,8192]{3,2,1,0:T(8,128)(2,1)}, bf16[2,16,512,512]{3,2,1,0:T(8,128)(2,1)}, f32[2,32,8192...) custom-call(bf16[2,16,32,8192]{3,2,1,0:T(8,128)(2,1)} %bitcast.9, ...), custom_call_target="tpu_custom_call" | custom-call | tf_op jit(solution)/shard_map/pallas_call | solution.py:306
  332.0 0.0 copy-start
  332.0 0.0 slice-start
  332.0 0.0 slice-start.1
  332.0 16.7 %copy.30 = bf16[2,512,8192]{2,1,0:T(8,128)(2,1)} copy(bf16[2,512,8192]{2,1,0:T(8,128)(2,1)} %bitcast.19) | data formatting | bytes 33554432
  348.7 0.0 copy-done
  348.7 0.0 slice-start.2
  348.7 0.0 slice-start.3
  348.7 8.5 %copy.31 = bf16[2,512,8192]{2,1,0:T(8,128)(2,1)} copy(bf16[2,512,8192]{2,1,0:T(8,128)(2,1)S(1)} %bitcast.18) | data formatting | bytes 33554432
  357.2 0.0 slice-done
  357.2 0.0 slice-done.1
  357.2 1.5 slice-done.2
  358.7 1.2 slice-done.3
  359.9 0.0 copy-start.6
  359.9 6.3 %copy.32 = bf16[2,8192,512]{2,1,0:T(8,128)(2,1)} copy(bf16[2,8192,512]{2,1,0:T(8,128)(2,1)S(1)} %bitcast.17) | data formatting | bytes 33554432
  366.2 0.0 copy-done.6
  366.2 0.0 copy-start.5
  366.2 1.3 copy.33
  367.5 1.0 copy-done.5
  368.5 0.0 copy-start.4
  368.5 1.3 copy.34
  369.8 1.0 copy-done.4
  370.9 0.0 copy-start.3
  370.9 1.3 copy.35
  372.2 1.0 copy-done.3
  373.2 0.0 copy-start.2
  373.2 1.3 copy.36
  374.5 1.0 copy-done.2
  375.6 0.0 copy-start.1
  375.6 1.3 copy.37
  376.9 1.0 copy-done.1
  377.9 1.3 copy.38
  (1 shorter events, 0.0 us)
Async XLA Ops:
  332.0 16.7 %copy-start = (bf16[2,16,32,8192]{3,2,1,0:T(8,128)(2,1)S(1)}, bf16[2,16,32,8192]{3,2,1,0:T(8,128)(2,1)}, u32[]{:S(2)}) copy-start(bf16[2,16,32,8192]{3,2,1,0:T(8,128)(2,1)} %get-tuple-element.19) | copy-start | bytes 50331652
  332.0 25.2 %slice-start = ((s8[16777216]{0:T(1024)(128)(4,1)}), s8[4194304]{0:T(1024)(128)(4,1)S(1)}, s32[]{:S(2)}) async-start(s8[16777216]{0:T(1024)(128)(4,1)} %bitcast.15), calls=%async_computation | async-start | bytes 8388608
  332.0 25.2 %slice-start.1 = ((s8[16777216]{0:T(1024)(128)(4,1)}), s8[4194304]{0:T(1024)(128)(4,1)S(1)}, s32[]{:S(2)}) async-start(s8[16777216]{0:T(1024)(128)(4,1)} %bitcast.15), calls=%async_computation.1 | async-start | bytes 8388608
  348.7 10.0 %slice-start.2 = ((s8[16777216]{0:T(1024)(128)(4,1)}), s8[4194304]{0:T(1024)(128)(4,1)S(1)}, s32[]{:S(2)}) async-start(s8[16777216]{0:T(1024)(128)(4,1)} %bitcast.15), calls=%async_computation.2 | async-start | bytes 8388608
  348.7 11.2 %slice-start.3 = ((s8[16777216]{0:T(1024)(128)(4,1)}), s8[4194304]{0:T(1024)(128)(4,1)S(1)}, s32[]{:S(2)}) async-start(s8[16777216]{0:T(1024)(128)(4,1)} %bitcast.15), calls=%async_computation.3 | async-start | bytes 8388608
  359.9 6.3 %copy-start.6 = (f32[2,32,8192]{2,1,0:T(8,128)S(1)}, f32[2,32,8192]{2,1,0:T(8,128)}, u32[]{:S(2)}) copy-start(f32[2,32,8192]{2,1,0:T(8,128)} %get-tuple-element.39) | copy-start | bytes 6291460
  366.2 2.3 copy-start.5
  368.5 2.3 copy-start.4
  370.9 2.3 copy-start.3
  373.2 2.3 copy-start.2
  375.6 2.3 copy-start.1

commit v2 on v1

v2 whole, which is shorter than its diff:
```python
import functools

import jax
import jax.numpy as jnp
from jax import lax
from jax.experimental import pallas as pl
from jax.experimental.pallas import tpu as pltpu
from jax.sharding import PartitionSpec as P

SUB = 8
LAYERS = 2
J = LAYERS * SUB
RING = 6
AHEAD = 2
STRIDE = {"x": 8, "y": 4, "z": 2}
ORDER = (("x", "y", "z"), ("y", "z", "x"), ("z", "x", "y"))
C = 3
F32, BF16 = jnp.float32, jnp.bfloat16
MESH = pl.DeviceIdType.MESH
D0, DN, S1, S2, S3, A1, A2, A3, FW = range(9)


def adamw(w, m, v, g):
    m = 0.9 * m + 0.1 * g
    v = 0.95 * v + 0.05 * g * g
    step = m * lax.rsqrt(v + 1e-8) + 0.1 * w
    return (w - 0.02 * step).astype(BF16), m, v


def place(c, b0, b1, b2, k):
    s = [STRIDE[d] for d in ORDER[c]]
    return b0 * s[0] + b1 * s[1] + b2 * s[2] + k


def part(c, j):
    layer, s = j // SUB, j % SUB
    if c < 2:
        width = 8192 // SUB
        return layer, slice(None), pl.ds(pl.multiple_of(s * width, width), width)
    height = 512 // SUB
    return layer, pl.ds(pl.multiple_of(s * height, height), height), slice(None)


def kernel(*refs):
    it = iter(refs)

    def take(n=C):
        return [next(it) for _ in range(n)]

    g, w, m, v = take(), take(), take(), take()
    r0, other, m_out, v_out = take(), take(), take(), take()
    r1, r2, r3 = take(), take(), take()
    o1, o2, o3, o4 = take(), take(), take(), take()
    mb, vb, wb = take(), take(), take()
    send, recv, load, moved = take(4)

    me = lax.axis_index("dp")
    core = me % 2
    bit = {d: me // s % 2 for d, s in STRIDE.items()}
    near = {d: me + s * (1 - 2 * bit[d]) for d, s in STRIDE.items()}
    partner = me + 1 - 2 * core
    mine = [tuple(bit[d] for d in ORDER[c]) for c in range(C)]

    def of_block(ref, c, blk, j):
        layer, rows, columns = part(c, j)
        return ref.at[layer, blk, rows, columns]

    def of_own(ref, c, j):
        layer, rows, columns = part(c, j)
        return ref.at[layer, rows, columns]

    def remote(c, j, group, src, dst, to):
        return pltpu.make_async_remote_copy(
            src_ref=src, dst_ref=dst, send_sem=send.at[group, c, j], recv_sem=recv.at[group, c, j], device_id={"dp": to}, device_id_type=MESH
        )

    def wait_for(ref, sem):
        pltpu.make_async_copy(ref, ref, sem).wait()

    def tiles(c, body, rows=32):
        if c < 2:
            across, down, high = 8192 // SUB // 512, 32 // rows, rows
        else:
            across, down = 1, 512 // SUB // rows

        @pl.loop(0, across * down)
        def _(i):
            row = pl.multiple_of(i % down * rows, rows)
            column = pl.multiple_of(i // down * 512, 512)
            body((pl.ds(row, rows), pl.ds(column, 512)))

    def start_exchange(j):
        for group in (D0, DN):
            for c in range(C):
                half = 1 - mine[c][0] if group == D0 else mine[c][0]
                for q in range(4):
                    blk = place(c, half, q // 2, q % 2, 1 - core)
                    remote(c, j, group, of_block(g[c], c, blk, j), r0[c].at[j, half * 4 + q], partner).start()

    def load_terms(stage, j):
        slot = j % 2
        for c in range(C):
            m0, m1, m2 = mine[c]
            if stage == 0:
                places = [(1 - m0, q // 2, q % 2) for q in range(4)]
            elif stage == 1:
                places = [(m0, 1 - m1, q) for q in range(2)]
            elif stage == 2:
                places = [(m0, m1, 1 - m2)]
            else:
                places = [(m0, m1, m2)]
            to = (o1, o2, o3, o4)[stage][c]
            for q, bits in enumerate(places):
                pltpu.make_async_copy(of_block(g[c], c, place(c, *bits, core), j), to.at[slot, q], load.at[stage, c, slot]).start()

    def load_own(j):
        slot = j % 2
        for c in range(C):

            @pl.when(j >= 2)
            def _():
                wait_for(mb[c].at[slot], moved.at[0, c, slot])
                wait_for(vb[c].at[slot], moved.at[1, c, slot])

            pltpu.make_async_copy(of_own(m[c], c, j), mb[c].at[slot], load.at[4, c, slot]).start()
            pltpu.make_async_copy(of_own(v[c], c, j), vb[c].at[slot], load.at[5, c, slot]).start()
            pltpu.make_async_copy(of_block(w[c], c, me, j), wb[c].at[slot], load.at[6, c, slot]).start()

    def stage1(j):
        slot = j % 2
        for c in range(C):
            m0, m1, m2 = mine[c]
            wait_for(r1[c].at[0], recv.at[D0, c, j])
            wait_for(o1[c].at[slot], load.at[0, c, slot])

            def body(at):
                for q in range(4):
                    p = (1 - m0) * 4 + q
                    r0[c][(j, p, *at)] = (r0[c][(j, p, *at)].astype(F32) + o1[c][(slot, q, *at)].astype(F32)).astype(BF16)

            tiles(c, body)
            remote(c, j, S1, r0[c].at[j, pl.ds((1 - m0) * 4, 4)], r1[c].at[j % RING], near[ORDER[c][0]]).start()

    def stage2(j):
        slot, ring = j % 2, j % RING
        for c in range(C):
            m0, m1, m2 = mine[c]
            wait_for(o2[c].at[slot], load.at[1, c, slot])
            wait_for(r1[c].at[0], recv.at[DN, c, j])
            wait_for(r1[c].at[0], recv.at[S1, c, j])
            wait_for(r1[c].at[0], send.at[S1, c, j])

            def body(at):
                for q in range(2):
                    p = (1 - m1) * 2 + q
                    total = r0[c][(j, m0 * 4 + p, *at)].astype(F32) + o2[c][(slot, q, *at)].astype(F32)
                    r1[c][(ring, p, *at)] = (total + r1[c][(ring, p, *at)].astype(F32)).astype(BF16)

            tiles(c, body)
            remote(c, j, S2, r1[c].at[ring, pl.ds((1 - m1) * 2, 2)], r2[c].at[ring], near[ORDER[c][1]]).start()

    def stage3(j):
        slot, ring = j % 2, j % RING
        for c in range(C):
            m0, m1, m2 = mine[c]
            wait_for(o3[c].at[slot], load.at[2, c, slot])
            wait_for(r2[c].at[0], recv.at[S2, c, j])
            wait_for(r2[c].at[0], send.at[S2, c, j])

            def body(at):
                p = 1 - m2
                total = r0[c][(j, m0 * 4 + m1 * 2 + p, *at)].astype(F32) + o3[c][(slot, 0, *at)].astype(F32)
                total = total + r1[c][(ring, m1 * 2 + p, *at)].astype(F32)
                r2[c][(ring, p, *at)] = (total + r2[c][(ring, p, *at)].astype(F32)).astype(BF16)

            tiles(c, body)
            remote(c, j, S3, r2[c].at[ring, pl.ds(1 - m2, 1)], r3[c].at[ring], near[ORDER[c][2]]).start()

    def give(c, j, p, n):
        remote(c, j, FW, r0[c].at[j, pl.ds(p, n)], other[c].at[j, pl.ds(p, n)], partner).start()

    def stage4(j):
        slot, ring = j % 2, j % RING
        for c in range(C):
            m0, m1, m2 = mine[c]
            here = m0 * 4 + m1 * 2 + m2
            wait_for(o4[c].at[slot], load.at[3, c, slot])
            wait_for(mb[c].at[slot], load.at[4, c, slot])
            wait_for(vb[c].at[slot], load.at[5, c, slot])
            wait_for(wb[c].at[slot], load.at[6, c, slot])
            wait_for(r3[c].at[0], recv.at[S3, c, j])
            wait_for(r3[c].at[0], send.at[S3, c, j])

            def body(at):
                total = r0[c][(j, here, *at)].astype(F32) + o4[c][(slot, 0, *at)].astype(F32)
                total = total + r1[c][(ring, m1 * 2 + m2, *at)].astype(F32)
                total = total + r2[c][(ring, m2, *at)].astype(F32)
                total = total + r3[c][(ring, 0, *at)].astype(F32)
                grad = total.astype(BF16).astype(F32)
                new = adamw(wb[c][(slot, *at)].astype(F32), mb[c][(slot, *at)], vb[c][(slot, *at)], grad)
                r0[c][(j, here, *at)], mb[c][(slot, *at)], vb[c][(slot, *at)] = new

            tiles(c, body, rows=16)
            remote(c, j, A1, r0[c].at[j, here], r0[c].at[j, here], near[ORDER[c][2]]).start()
            pltpu.make_async_copy(mb[c].at[slot], of_own(m_out[c], c, j), moved.at[0, c, slot]).start()
            pltpu.make_async_copy(vb[c].at[slot], of_own(v_out[c], c, j), moved.at[1, c, slot]).start()
            give(c, j, here, 1)

    def stage5(j):
        for c in range(C):
            m0, m1, m2 = mine[c]
            pair = m0 * 4 + m1 * 2
            wait_for(r3[c].at[0], recv.at[A1, c, j])
            remote(c, j, A2, r0[c].at[j, pl.ds(pair, 2)], r0[c].at[j, pl.ds(pair, 2)], near[ORDER[c][1]]).start()
            give(c, j, pair + 1 - m2, 1)

    def stage6(j):
        for c in range(C):
            m0, m1, m2 = mine[c]
            wait_for(r2[c].at[0], recv.at[A2, c, j])
            remote(c, j, A3, r0[c].at[j, pl.ds(m0 * 4, 4)], r0[c].at[j, pl.ds(m0 * 4, 4)], near[ORDER[c][0]]).start()
            give(c, j, m0 * 4 + (1 - m1) * 2, 2)

    def stage7(j):
        for c in range(C):
            m0, m1, m2 = mine[c]
            wait_for(r1[c].at[0], recv.at[A3, c, j])
            give(c, j, (1 - m0) * 4, 4)

    barrier = pltpu.get_barrier_semaphore()
    for to in (partner, *near.values()):
        pl.semaphore_signal(barrier, inc=1, device_id={"dp": to}, device_id_type=MESH)
    pl.semaphore_wait(barrier, 4)

    for j in range(AHEAD):
        start_exchange(j)
    load_terms(0, 0)

    @pl.loop(0, J + 6)
    def _(t):
        def on(j, run):
            pl.when(jnp.logical_and(j >= 0, j < J))(lambda: run(j))

        on(t + AHEAD, start_exchange)
        on(t + 1, functools.partial(load_terms, 0))
        on(t, functools.partial(load_terms, 1))
        on(t - 1, functools.partial(load_terms, 2))
        on(t - 2, functools.partial(load_terms, 3))
        on(t - 2, load_own)
        for back, stage in enumerate((stage1, stage2, stage3, stage4, stage5, stage6, stage7)):
            on(t - back, stage)

    for c in range(C):
        for slot in range(2):
            wait_for(mb[c].at[slot], moved.at[0, c, slot])
            wait_for(vb[c].at[slot], moved.at[1, c, slot])

    @pl.loop(0, J)
    def _(j):
        for c in range(C):
            wait_for(r1[c].at[0], send.at[D0, c, j])
            wait_for(r1[c].at[0], send.at[DN, c, j])
            wait_for(r3[c].at[0], send.at[A1, c, j])
            wait_for(r2[c].at[0], send.at[A2, c, j])
            wait_for(r1[c].at[0], send.at[A3, c, j])
            wait_for(r0[c].at[j], send.at[FW, c, j])
            wait_for(r0[c].at[j], recv.at[FW, c, j])


def write_out(*refs):
    it = iter(refs)
    held = [[next(it) for _ in range(C)] for _ in range(2)]
    moments = [next(it) for _ in range(2 * C)]
    out = [next(it) for _ in range(C)]
    moments_out = [next(it) for _ in range(2 * C)]
    between = [next(it) for _ in range(2 * C)]
    sem, load, store = it
    core = lax.axis_index("dp") % 2

    for i in range(2 * C):
        pltpu.make_async_copy(moments[i], between[i], load.at[i]).start()

    @pl.loop(0, J)
    def _(j):
        for who in range(2):
            for c in range(C):
                for p in range(8):
                    blk = place(c, p // 4, p // 2 % 2, p % 2, core if who == 0 else 1 - core)
                    layer, rows, columns = part(c, j)
                    pltpu.make_async_copy(held[who][c].at[j, p], out[c].at[layer, blk, rows, columns], sem.at[who, c, j]).start()

    for i in range(2 * C):
        pltpu.make_async_copy(moments[i], between[i], load.at[i]).wait()
        pltpu.make_async_copy(between[i], moments_out[i], store.at[i]).start()

    @pl.loop(0, J)
    def _(j):
        for who in range(2):
            for c in range(C):
                pltpu.make_async_copy(held[who][c].at[j], held[who][c].at[j], sem.at[who, c, j]).wait()

    for i in range(2 * C):
        pltpu.make_async_copy(between[i], moments_out[i], store.at[i]).wait()


def solution(mesh):
    chunk = ((32, 8192 // SUB),) * 2 + ((512 // SUB, 512),)
    blocks = ((LAYERS, 16, 32, 8192),) * 2 + ((LAYERS, 16, 512, 512),)
    own = ((LAYERS, 32, 8192),) * 2 + ((LAYERS, 512, 512),)
    whole = ((LAYERS, 512, 8192),) * 2 + ((LAYERS, 8192, 512),)

    def vmem(*lead, dtype=BF16):
        return [pltpu.VMEM((*lead, *chunk[c]), dtype) for c in range(C)]

    anywhere, resident = pl.BlockSpec(memory_space=pl.ANY), pl.BlockSpec(memory_space=pltpu.VMEM)
    moments = [jax.ShapeDtypeStruct(s, F32) for s in own] * 2
    call = pl.pallas_call(
        kernel,
        out_shape=[*vmem(J, 8), *vmem(J, 8), *moments],
        in_specs=[anywhere] * 12,
        out_specs=[resident] * 6 + [anywhere] * 6,
        scratch_shapes=[
            *vmem(RING, 4),
            *vmem(RING, 2),
            *vmem(RING, 1),
            *vmem(2, 4),
            *vmem(2, 2),
            *vmem(2, 1),
            *vmem(2, 1),
            *vmem(2, dtype=F32),
            *vmem(2, dtype=F32),
            *vmem(2),
            pltpu.SemaphoreType.DMA((9, C, J)),
            pltpu.SemaphoreType.DMA((9, C, J)),
            pltpu.SemaphoreType.DMA((7, C, 2)),
            pltpu.SemaphoreType.DMA((2, C, 2)),
        ],
        compiler_params=pltpu.CompilerParams(collective_id=0, has_side_effects=True, vmem_limit_bytes=14 << 20),
    )
    finish = pl.pallas_call(
        write_out,
        out_shape=[jax.ShapeDtypeStruct(s, BF16) for s in blocks] + moments,
        in_specs=[resident] * 6 + [anywhere] * 6,
        out_specs=[anywhere] * 9,
        scratch_shapes=[
            *[pltpu.VMEM(s, F32) for s in own * 2],
            pltpu.SemaphoreType.DMA((2, C, J)),
            pltpu.SemaphoreType.DMA((2 * C,)),
            pltpu.SemaphoreType.DMA((2 * C,)),
        ],
        compiler_params=pltpu.CompilerParams(vmem_limit_bytes=14 << 20),
    )

    def step(*arrays):
        terms = [a.reshape(s) for a, s in zip(arrays[:3], blocks, strict=True)]
        weights = [a.reshape(s) for a, s in zip(arrays[3:6], blocks, strict=True)]
        kept = call(*terms, *weights, *arrays[6:])
        new = finish(*[pltpu.with_memory_space_constraint(a, pltpu.VMEM) for a in kept[:6]], *kept[6:])
        return (*(a.reshape(s) for a, s in zip(new[:3], whole, strict=True)), *new[3:])

    all_of, cut = P(None, None, None), P(None, "dp", None)
    return jax.shard_map(
        step,
        mesh=mesh,
        in_specs=(P(("rep", "dp"), None, None, None),) * 3 + (all_of,) * 3 + (cut,) * 6,
        out_specs=(P("rep", None, None),) * 3 + (P("rep", "dp", None),) * 6,
        check_vma=False,
    )
```

time: 380 us -> 357 us (0.939)
  local copies, waits for them, and re-layouts: 47.2 us -> 0 us
  Pallas kernels: 331 us -> 356 us
    unnamed x31 -> x0, local copies, waits for them, and re-layouts: 47.2 us -> none
    pallas_call x1 -> x2, Pallas kernels: 331 us -> 356 us  [the longest x1 332 us: step(): kept = call(*terms, *weights, *arrays[6:])]
where the time goes in v2:
time: 357 us
  Pallas kernels  356 us (100%)
    pallas_call x1, Pallas kernels, step(): kept = call(*terms, *weights, *arrays[6:])  332 us
    pallas_call x1, Pallas kernels, step(): finish(*[pltpu.with_memory_space_constraint(a, pltpu.VMEM) for a in kept[...  24.3 us

profile of v2, /device:TPU:0, one launch (start us, length us, event | category | flops | bytes accessed | tf_op | source)
XLA Modules:
  0.0 357.0 jit_solution(16281040002317001838)
XLA Ops:
  0.6 332.1 %shard_map.187 = (bf16[16,8,32,1024]{3,2,1,0:T(8,128)(2,1)S(1)}, bf16[16,8,32,1024]{3,2,1,0:T(8,128)(2,1)S(1)}, bf16[16,8,64,512]{3,2,1,0:T(8,128)(2,1)S(1)}, bf...) custom-call(bf16[2,16,32,8192]{3,2,1,0:T(8,128)(2,1)} %bitcast.9, ...), custom_call_target="tpu_custom_call" | custom-call | tf_op jit(solution)/shard_map/pallas_call | solution.py:357
  332.7 24.3 %shard_map.188 = (bf16[2,16,32,8192]{3,2,1,0:T(8,128)(2,1)}, bf16[2,16,32,8192]{3,2,1,0:T(8,128)(2,1)}, bf16[2,16,512,512]{3,2,1,0:T(8,128)(2,1)}, f32[2,32,8192...) custom-call(bf16[16,8,32,1024]{3,2,1,0:T(8,128)(2,1)S(1)} %get-tuple, ...), custom_call_target="tpu_custom_call" | custom-call | tf_op jit(solution)/shard_map/pallas_call | solution.py:358
